TPU v7x, 32 devices: a whole 2x2x4 slice. The times are simulated.
32 devices in a mesh: section: 2 (over core), dp: 16 (over z, y, x).
Axes of the slice: x: 2, y: 2, z: 4, core: 2. Of those that a mesh axis runs over, the one named last changes fastest.
Arguments:
- tokens: bfloat16 [2, 16, 80, 1024], P(None, 'dp'), may hold values from -6 to 6
- w_qkv: bfloat16 [2, 1024, 1536], P('section', 'dp'), may hold values from -0.1875 to 0.1875
- w_output: bfloat16 [2, 512, 1024], P('section', None, 'dp'), may hold values from -0.25 to 0.25
- tangent_value: bfloat16 [2, 2, 1024, 512], P('section', None, 'dp'), may hold values from -0.1875 to 0.1875
- tangent_output: bfloat16 [2, 2, 512, 1024], P('section', None, None, 'dp'), may hold values from -0.25 to 0.25
- layer_gain: float32 [2, 1024], P('section'), may hold values from 0.5 to 1.5
- final_gain: float32 [1024], replicated, may hold values from 0.5 to 1.5
- head: bfloat16 [1024, 1000], P(None, 'section'), may hold values from -0.1875 to 0.1875
Outputs:
- mean_logits: float32 [2, 16, 1000], P(None, 'dp', 'section')
- variance: float32 [2, 16, 1000], P(None, 'dp', 'section')
All inputs are finite; a program needn't handle non-finite values.
Results may differ from a plain program's by a relative error of at most 0.018.
Values may be sent and summed in bfloat16 or wider, within the bound.
A program may use at most 64 MiB of HBM per device.

v0:
```python
import jax
import jax.numpy as jnp
from jax import lax
from jax.sharding import PartitionSpec as P

HEADS = 8
HEAD = 64
TANGENTS = 2
HD = 512


epsilon = 1e-06


def passed_along(block, axis, distance):
    devices = range(lax.axis_size(axis))
    route = [(i - distance, i) for i in devices if i - distance in devices]
    return lax.ppermute(block, axis, route)


def spread(shard, axis, root):
    mine = lax.axis_index(axis) == root
    return lax.psum(jnp.where(mine, shard, jnp.zeros_like(shard)), axis)


def contract(spec, left, right):
    return jnp.einsum(spec, left, right, preferred_element_type=jnp.float32)


def norm_jvp(primal, tangents, gains):
    average = jnp.mean(primal, -1, keepdims=True)
    centred = primal - average
    inverse = lax.rsqrt(jnp.mean(centred * centred, -1, keepdims=True) + epsilon)
    dcentred = tangents - jnp.mean(tangents, -1, keepdims=True)
    dinverse = -(inverse**3) * jnp.mean(centred * dcentred, -1, keepdims=True)
    return (centred * inverse * gains, (dcentred * inverse + centred * dinverse) * gains)


def layer_step(state, qkv_weight, out_weight, value_tangent, out_tangent, gains):
    resid = state.astype(jnp.float32)
    normed_zero, normed_rest = norm_jvp(resid[0], resid[1:], gains)
    normed = jnp.concatenate([normed_zero[None], normed_rest]).astype(jnp.bfloat16)
    streams, batch, tokens_here, width = normed.shape
    projected = contract("sbtd,de->sbte", normed, qkv_weight)
    extra_value = contract("btd,kde->kbte", normed[0], value_tangent)
    queries = projected[..., :HD]
    key_rows = projected[..., HD : 2 * HD]
    values = projected[..., 2 * HD :]
    values = jnp.concatenate([values[:1], values[1:] + extra_value])
    shape_heads = (streams, batch, tokens_here, HEADS, HEAD)
    queries = queries.astype(jnp.bfloat16).reshape(shape_heads)
    key_rows = key_rows.astype(jnp.bfloat16).reshape(shape_heads)
    values = values.astype(jnp.bfloat16).reshape(shape_heads)
    factor = HEAD ** (-0.5)
    scores = contract("bqhe,bkhe->bhqk", queries[0], key_rows[0]) * factor
    probs = jax.nn.softmax(scores, -1)
    dscores = (
        contract("sbqhe,bkhe->sbhqk", queries[1:], key_rows[0])
        + contract("bqhe,sbkhe->sbhqk", queries[0], key_rows[1:])
    ) * factor
    dprobs = probs * (dscores - jnp.sum(probs * dscores, -1, keepdims=True))
    probs_low = probs.astype(jnp.bfloat16)
    dprobs_low = dprobs.astype(jnp.bfloat16)
    attended_zero = contract("bhqk,bkhe->bqhe", probs_low, values[0])
    attended_rest = contract("sbhqk,bkhe->sbqhe", dprobs_low, values[0]) + contract(
        "bhqk,sbkhe->sbqhe", probs_low, values[1:]
    )
    attended = jnp.concatenate([attended_zero[None], attended_rest]).astype(jnp.bfloat16)
    attended = attended.reshape(streams, batch, tokens_here, HD)
    output = contract("sbte,ed->sbtd", attended, out_weight)
    extra_out = contract("bte,ked->kbtd", attended[0], out_tangent)
    output = jnp.concatenate([output[:1], output[1:] + extra_out])
    return (resid + output).astype(jnp.bfloat16)


def shards(tokens, w_qkv, w_output, tangent_value, tangent_output, layer_gain, final_gain, head):
    full_qkv, full_output, full_value_tan, full_output_tan = (
        lax.all_gather(w_qkv, "dp", axis=1, tiled=True),
        lax.all_gather(w_output, "dp", axis=2, tiled=True),
        lax.all_gather(tangent_value, "dp", axis=2, tiled=True),
        lax.all_gather(tangent_output, "dp", axis=3, tiled=True),
    )
    section_gain = layer_gain[0]

    def advance_layer(state):
        return layer_step(
            state, full_qkv[0], full_output[0], full_value_tan[0], full_output_tan[0], section_gain
        )

    def blank_layer(state):
        return jnp.zeros_like(state)

    section_index = lax.axis_index("section")
    section_count = lax.axis_size("section")
    micro_count = tokens.shape[0]
    image_tokens = tokens.shape[2]
    model_width = tokens.shape[3]
    flat_tokens = tokens.reshape(micro_count, image_tokens, model_width)
    entering = jnp.concatenate(
        [
            flat_tokens[None],
            jnp.zeros((TANGENTS, micro_count, image_tokens, model_width), jnp.bfloat16),
        ]
    )

    def advance(step, outgoing):
        incoming = passed_along(outgoing, "section", 1)
        source = jnp.where(step == 0, entering, incoming)
        return lax.cond(section_index == step, advance_layer, blank_layer, source)

    finished = lax.fori_loop(0, section_count, advance, jnp.zeros_like(entering))
    collected = finished[:, :, 0, :]
    features = spread(collected, "section", section_count - 1)
    widened = features.astype(jnp.float32)
    final_zero, final_rest = norm_jvp(widened[0], widened[1:], final_gain)
    normed_final = jnp.concatenate([final_zero[None], final_rest]).astype(jnp.bfloat16)
    logits = contract("sbd,dc->sbc", normed_final, head)
    mean_logits = logits[0][:, None, :]
    variance = jnp.sum(logits[1:] * logits[1:], 0)[:, None, :]
    return (mean_logits, variance)


def solution(mesh):
    return jax.shard_map(
        shards,
        mesh=mesh,
        in_specs=(
            P(None, "dp", None, None),
            P("section", "dp", None),
            P("section", None, "dp"),
            P("section", None, "dp", None),
            P("section", None, None, "dp"),
            P("section", None),
            P(),
            P(None, "section"),
        ),
        out_specs=(P(None, "dp", "section"), P(None, "dp", "section")),
        check_vma=False,
    )
```

profile of v0, /device:TPU:0, one launch (start us, length us, event | category | flops | bytes accessed | tf_op | source)
XLA Modules:
  0.0 363.6 jit_solution(397658022795245036)
XLA Ops:
  8.0 1.7 copy.64
  11.0 2.1 concatenate.31
  13.1 55.5 %all-gather.9.cloned.1.call-done = bf16[1,512,1024]{1,2,0:T(8,128)(2,1)} async-done(((bf16[1,512,64]{1,2,0:T(8,128)(2,1)}), bf16[1,512,1024]{1,2,0:T(8,128)(2,1)}) %all-gather.9.cloned.1.call-update) | async-done | bytes 1048592 | tf_op jit(solution)/shard_map/all_gather | solution.py:79
  68.6 2.3 copy.65
  70.9 59.7 %all-gather.11.cloned.1.call-done = bf16[1,2,512,1024]{2,1,0,3:T(2,128)(2,1)} async-done(((bf16[1,2,512,64]{2,1,0,3:T(2,128)(2,1)}), bf16[1,2,512,1024]{2,1,0,3:T(2,128)(2,1)}) %all-gather.11.cloned.1.call-update) | async-done | bytes 2097168 | tf_op jit(solution)/shard_map/all_gather | solution.py:81
  130.6 6.2 %copy.66 = bf16[1,2,512,1024]{3,2,1,0:T(8,128)(2,1)} copy(bf16[1,2,512,1024]{2,1,0,3:T(2,128)(2,1)} %all-gather.11.cloned.1.call-done) | data formatting | bytes 4194304 | tf_op jit(solution)/shard_map/while | solution.py:111
  136.8 55.8 %all-gather.7.cloned.1.call-done = bf16[1,2,1024,512]{3,2,1,0:T(8,128)(2,1)} async-done(((bf16[1,2,64,512]{3,2,1,0:T(8,128)(2,1)}), bf16[1,2,1024,512]{3,2,1,0:T(8,128)(2,1)}) %all-gather.7.cloned.1.call-update) | async-done | bytes 2097168 | tf_op jit(solution)/shard_map/all_gather | solution.py:80
  192.5 69.3 %all-gather.5.cloned.1.call-done = bf16[1,1024,1536]{2,1,0:T(8,128)(2,1)} async-done(((bf16[1,64,1536]{2,1,0:T(8,128)(2,1)}), bf16[1,1024,1536]{2,1,0:T(8,128)(2,1)}) %all-gather.5.cloned.1.call-update) | async-done | bytes 3145744 | tf_op jit(solution)/shard_map/all_gather | solution.py:78
  262.9 47.7 %while.13 = (s32[]{:T(128)}, bf16[3,2,80,1024]{3,2,1,0:T(8,128)(2,1)}, s32[]{:T(128)}, bf16[3,2,80,1024]{3,2,1,0:T(8,128)(2,1)}, f32[1,1024]{1,0:T(1,128)S(1)}, ...) while((s32[]{:T(128)}, ...), condition=%wide.region_10.11_spmd, body=%wide.region_0.10_spmd.sunk | while | flops 2827160064 | bytes 100394192 | solution.py:111
  262.9 1.3 collective-permute-start
  264.2 2.3 collective-permute-done
  266.5 39.3 %conditional.2 = (bf16[3,2,80,1024]{3,2,1,0:T(8,128)(2,1)}) conditional(s32[]{:T(128)} %convert_element_type.51, () %tuple.55, (s32[]{:T(128)}, bf16[3,2,80,1024]{3,2,1,0:T(8,128)(2,1)}, bf16[3,2,80,1024]{3,2,1,0:T(8,128)(2,1)S(1)}, f32[1,1024]{1,0:T(1,128)S(1)}, bf16[1,1024,1536]{2,1,0:T(8,128)(2,1)}, /*index=5*/bf16[1,2,1024,512]{3,2,1,0:T(8,128)(2,1)}, ...), branch_computations={%region_1.1_spmd, %region_2.9_spmd} | conditional | flops 2827160064 | bytes 96461808 | solution.py:109
  267.5 1.3 select_convert_fusion
  270.3 1.2 copy-done.10
  271.5 2.9 fusion.83
  274.9 1.2 slice.90
  277.2 1.9 fusion.81
  281.2 2.2 slice.87
  283.4 2.2 slice.85
  285.6 2.9 convolution_bitcast_fusion.1
  288.5 2.3 fusion.84
  290.8 1.3 broadcast_multiply_fusion
  292.5 1.4 multiply_reduce_fusion
  295.0 1.2 fusion.17
  297.2 2.2 copy.61
  299.4 2.2 concatenate.26
  301.8 2.1 fusion.28
  304.6 1.3 fusion.7
  305.9 1.3 collective-permute-start
  307.2 2.3 collective-permute-done
  310.6 2.1 copy.67
  312.7 41.8 %psum.7 = bf16[3,2,1024]{2,0,1:T(4,128)(2,1)S(1)} all-reduce(bf16[3,2,1024]{2,0,1:T(4,128)(2,1)S(1)} %fusion.71), channel_id=1, replica_groups=mesh['section'=2,'dp'=16] {'section'}, use_global_device_ids=true, to_apply=%region_11.12 | all-reduce | flops 6144 | bytes 24576 | tf_op jit(solution)/shard_map/psum | solution.py:23
  (70 shorter events, 16.9 us)
Async XLA Ops:
  7.2 348.2 %copy-start = (bf16[1024,500]{0,1:T(8,128)(2,1)S(1)}, bf16[1024,500]{0,1:T(8,128)(2,1)}, u32[]{:S(2)}) copy-start(bf16[1024,500]{0,1:T(8,128)(2,1)} %param.19) | copy-start | bytes 3072004
  7.2 61.4 %all-gather.9.cloned.1.call-start = ((), (), s32[]{:S(2)}) async-start(), calls=%async_computation.2 | async-start | bytes 1114112 | tf_op jit(solution)/shard_map/all_gather | solution.py:79
  7.9 122.7 %all-gather.11.cloned.1.call-start = ((), (), s32[]{:S(2)}) async-start(), calls=%async_computation.3 | async-start | bytes 2228224 | tf_op jit(solution)/shard_map/all_gather | solution.py:81
  9.7 182.8 %all-gather.7.cloned.1.call-start = ((), (), s32[]{:S(2)}) async-start(), calls=%async_computation.1 | async-start | bytes 2228224 | tf_op jit(solution)/shard_map/all_gather | solution.py:80
  10.4 251.4 %all-gather.5.cloned.1.call-start = ((), (), s32[]{:S(2)}) async-start(), calls=%async_computation | async-start | bytes 3342336 | tf_op jit(solution)/shard_map/all_gather | solution.py:78
  70.9 192.0 %copy-start.8 = (f32[1,1024]{1,0:T(1,128)S(1)}, f32[1,1024]{1,0:T(1,128)}, u32[]{:S(2)}) copy-start(f32[1,1024]{1,0:T(1,128)} %param.17) | copy-start | bytes 12292
  262.9 3.7 %collective-permute-start = (bf16[3,2,80,1024]{3,2,1,0:T(8,128)(2,1)}, bf16[3,2,80,1024]{3,2,1,0:T(8,128)(2,1)S(1)}, u32[]{:S(2)}, u32[]{:S(2)}) collective-permute-start(bf16[3,2,80,1024]{3,2,1,0:T(8,128)(2,1)} %get-tuple-element.322), channel_id=1, source_target_pairs={{0,16},{1,17},{2,18},{3,19},{4,20},{5,21},{6,22},{7,23},{8,24},{9,... | collective-permute-start | bytes 2949128 | tf_op jit(solution)/shard_map/while/body/eval_jaxpr/ppermute | solution.py:18
  266.5 0.9 copy-start.7
  269.6 1.9 copy-start.10
  271.5 2.9 copy-start.6
  290.8 1.5 copy-start.1
  290.8 1.7 copy-start.4
  293.9 1.1 copy-start.3
  297.2 4.5 %copy-start.5 = (bf16[2,8,64,80]{3,2,1,0:T(8,128)(2,1)S(1)}, bf16[2,8,64,80]{3,2,1,0:T(8,128)(2,1)}, u32[]{:S(2)}) copy-start(bf16[2,8,64,80]{3,2,1,0:T(8,128)(2,1)} %convolution_convert_fusion) | copy-start | bytes 491524 | tf_op jit(solution)/shard_map/while/body/eval_jaxpr/cond
  301.8 2.2 copy-start.2
  305.9 3.7 %collective-permute-start = (bf16[3,2,80,1024]{3,2,1,0:T(8,128)(2,1)}, bf16[3,2,80,1024]{3,2,1,0:T(8,128)(2,1)S(1)}, u32[]{:S(2)}, u32[]{:S(2)}) collective-permute-start(bf16[3,2,80,1024]{3,2,1,0:T(8,128)(2,1)} %get-tuple-element.322), channel_id=1, source_target_pairs={{0,16},{1,17},{2,18},{3,19},{4,20},{5,21},{6,22},{7,23},{8,24},{9,... | collective-permute-start | bytes 2949128 | tf_op jit(solution)/shard_map/while/body/eval_jaxpr/ppermute | solution.py:18
  310.6 44.4 %copy-start.9 = (f32[1024]{0:T(1024)S(1)}, f32[1024]{0:T(1024)}, u32[]{:S(2)}) copy-start(f32[1024]{0:T(1024)} %param.18) | copy-start | bytes 12292
Sparse Core Ops, SparseCore 0:
  10.7 57.7 all-gather.8
  71.4 59.2 all-gather.10
  133.4 59.1 all-gather.6
  195.2 66.5 all-gather.4
where the time goes:
time: 364 us
  waiting for transfers between devices  247 us (68%)
  blocking collectives  41.8 us (11%)
  local copies, waits for them, and re-layouts  36.2 us (10%)
  matrix products  15.6 us (4%)
  between operations  13.8 us (4%)
  other arithmetic  6.18 us (2%)
    all_gather x1, waiting for transfers between devices, shards(): lax.all_gather(w_qkv, 'dp', axis=1, tiled=True)  69.3 us
    all_gather x1, waiting for transfers between devices, shards(): lax.all_gather(tangent_output, 'dp', axis=3, tiled=True)  59.7 us
    all_gather x1, waiting for transfers between devices, shards(): lax.all_gather(tangent_value, 'dp', axis=2, tiled=True)  55.8 us
    all_gather x1, waiting for transfers between devices, shards(): lax.all_gather(w_output, 'dp', axis=2, tiled=True)  55.5 us
    psum x1, blocking collectives, spread(): return lax.psum(jnp.where(mine, shard, jnp.zeros_like(shard)), axis)  41.8 us
    dot_general x10, matrix products, contract(): return jnp.einsum(spec, left, right, preferred_element_type=jnp.float32)  13.3 us
    while x3, local copies, waits for them, and re-layouts, shards(): lax.fori_loop(0, section_count, advance, jnp.zeros_like(entering))  10.5 us
  transfers between devices with their start and end apart: 6, of which 6 were waited for; matrix products, arithmetic and copies ran while one was open for 3% of the time, Pallas kernels for 0%

commit v1 on v0

v1 whole, which is shorter than its diff:
```python
import functools

import jax
import jax.numpy as jnp
from jax import lax
from jax.experimental import pallas as pl
from jax.experimental.pallas import tpu as pltpu
from jax.sharding import PartitionSpec as P

HEAD = 64
epsilon = 1e-06
F32, BF16 = jnp.float32, jnp.bfloat16
MESH = pl.DeviceIdType.MESH


def contract(spec, left, right):
    return jnp.einsum(spec, left, right, preferred_element_type=jnp.float32)


def norm_jvp(primal, tangents, gains):
    average = jnp.mean(primal, -1, keepdims=True)
    centred = primal - average
    inverse = lax.rsqrt(jnp.mean(centred * centred, -1, keepdims=True) + epsilon)
    dcentred = tangents - jnp.mean(tangents, -1, keepdims=True)
    dinverse = -(inverse**3) * jnp.mean(centred * dcentred, -1, keepdims=True)
    return (centred * inverse * gains, (dcentred * inverse + centred * dinverse) * gains)


def layer_step(state, qkv_weight, out_weight, value_tangent, out_tangent, gains):
    hd = out_weight.shape[0]
    heads = hd // HEAD
    resid = state.astype(F32)
    normed_zero, normed_rest = norm_jvp(resid[0], resid[1:], gains)
    normed = jnp.concatenate([normed_zero[None], normed_rest]).astype(BF16)
    streams, batch, tokens_here, width = normed.shape
    projected = contract("sbtd,de->sbte", normed, qkv_weight)
    extra_value = contract("btd,kde->kbte", normed[0], value_tangent)
    queries = projected[..., :hd]
    key_rows = projected[..., hd : 2 * hd]
    values = projected[..., 2 * hd :]
    values = jnp.concatenate([values[:1], values[1:] + extra_value])
    shape_heads = (streams, batch, tokens_here, heads, HEAD)
    queries = queries.astype(BF16).reshape(shape_heads)
    key_rows = key_rows.astype(BF16).reshape(shape_heads)
    values = values.astype(BF16).reshape(shape_heads)
    factor = HEAD ** (-0.5)
    scores = contract("bqhe,bkhe->bhqk", queries[0], key_rows[0]) * factor
    probs = jax.nn.softmax(scores, -1)
    dscores = (
        contract("sbqhe,bkhe->sbhqk", queries[1:], key_rows[0])
        + contract("bqhe,sbkhe->sbhqk", queries[0], key_rows[1:])
    ) * factor
    dprobs = probs * (dscores - jnp.sum(probs * dscores, -1, keepdims=True))
    probs_low = probs.astype(BF16)
    dprobs_low = dprobs.astype(BF16)
    attended_zero = contract("bhqk,bkhe->bqhe", probs_low, values[0])
    attended_rest = contract("sbhqk,bkhe->sbqhe", dprobs_low, values[0]) + contract(
        "bhqk,sbkhe->sbqhe", probs_low, values[1:]
    )
    attended = jnp.concatenate([attended_zero[None], attended_rest]).astype(BF16)
    attended = attended.reshape(streams, batch, tokens_here, hd)
    output = contract("sbte,ed->sbtd", attended, out_weight)
    extra_out = contract("bte,ked->kbtd", attended[0], out_tangent)
    output = jnp.concatenate([output[:1], output[1:] + extra_out])
    return (resid + output).astype(BF16)


def relay_shards(tokens, w_qkv, w_output, tangent_value, tangent_output, layer_gain, final_gain, head):
    full_qkv, full_output, full_value_tan, full_output_tan = (
        lax.all_gather(w_qkv, "dp", axis=1, tiled=True),
        lax.all_gather(w_output, "dp", axis=2, tiled=True),
        lax.all_gather(tangent_value, "dp", axis=2, tiled=True),
        lax.all_gather(tangent_output, "dp", axis=3, tiled=True),
    )
    tangents = tangent_value.shape[1]

    def advance_layer(state):
        return layer_step(
            state, full_qkv[0], full_output[0], full_value_tan[0], full_output_tan[0], layer_gain[0]
        )

    section_index = lax.axis_index("section")
    section_count = lax.axis_size("section")
    route = [(i, i + 1) for i in range(section_count - 1)]
    micro, _, toks, width = tokens.shape
    entering = jnp.concatenate(
        [tokens.reshape(1, micro, toks, width), jnp.zeros((tangents, micro, toks, width), BF16)]
    )

    def advance(step, outgoing):
        incoming = lax.ppermute(outgoing, "section", route)
        source = jnp.where(step == 0, entering, incoming)
        return lax.cond(section_index == step, advance_layer, jnp.zeros_like, source)

    finished = lax.fori_loop(0, section_count, advance, jnp.zeros_like(entering))
    collected = finished[:, :, 0, :]
    mine = section_index == section_count - 1
    features = lax.psum(jnp.where(mine, collected, jnp.zeros_like(collected)), "section")
    widened = features.astype(F32)
    final_zero, final_rest = norm_jvp(widened[0], widened[1:], final_gain)
    normed_final = jnp.concatenate([final_zero[None], final_rest]).astype(BF16)
    logits = contract("sbd,dc->sbc", normed_final, head)
    return (logits[0][:, None, :], jnp.sum(logits[1:] * logits[1:], 0)[:, None, :])


def dot(a, b):
    return lax.dot_general(a, b, (((1,), (0,)), ((), ())), preferred_element_type=F32)


def dot_t(a, b):
    return lax.dot_general(a, b, (((1,), (1,)), ((), ())), preferred_element_type=F32)


class Gather:
    def __init__(self, n, a_full, b_full, send, recv):
        self.nz = n // 4
        self.a_full, self.b_full, self.send, self.recv = a_full, b_full, send, recv
        self.rows = a_full.shape[0] // n
        self.me = lax.axis_index("dp")
        self.section = lax.axis_index("section")
        me = self.me
        self.x_near = me + 1 - 2 * (me % 2)
        self.y_near = me + 2 - 4 * ((me // 2) % 2)
        self.z = me // 4
        self.diagonal = self.x_near + self.y_near - me
        self.sends = []
        self.slot = 0

    def piece(self, src, group, half):
        depth = self.rows // 2
        at = pl.ds(pl.multiple_of(src * self.rows + half * depth, depth), depth)
        return self.a_full.at[at, :] if group == 0 else self.b_full.at[:, at, :]

    def copy(self, src, group, half, target, slot):
        ref = self.piece(src, group, half)
        return pltpu.make_async_remote_copy(
            src_ref=ref,
            dst_ref=ref,
            send_sem=self.send.at[slot],
            recv_sem=self.recv.at[src, group * 2 + half],
            device_id={"section": self.section, "dp": target},
            device_id_type=MESH,
        )

    def forward(self, cond, src, group, half, target):
        slot = self.slot
        self.slot += 1

        def go():
            self.copy(src, group, half, target, slot).start()

        def end():
            self.copy(src, group, half, target, slot).wait_send()

        if cond is None:
            go()
        else:
            pl.when(cond)(go)
        self.sends.append((cond, end))

    def arrived(self, src, group, half):
        self.copy(src, group, half, self.me, 0).wait_recv()

    def sources(self, d):
        if d == 0:
            return [(0, None)]
        return [(-d, self.z >= d), (d, self.z + d < self.nz)]

    def direct(self, group, d):
        for shift, cond in self.sources(d):
            src = self.me + 4 * shift
            for half in range(2):
                if d > 0:
                    pl.when(cond)(functools.partial(self.arrived, src, group, half))
                if shift <= 0 and d < self.nz - 1:
                    up = self.z + 1 < self.nz
                    self.forward(up if cond is None else cond & up, src, group, half, self.me + 4)
                if shift >= 0 and d < self.nz - 1:
                    down = self.z >= 1
                    self.forward(down if cond is None else cond & down, src, group, half, self.me - 4)
                order = ((self.y_near, self.x_near), (self.x_near, self.y_near))[half]
                for target in order:
                    self.forward(cond, src, group, half, target)

    def relay(self, group, d):
        for shift, cond in self.sources(d):
            for half, near, target in ((0, self.x_near, self.y_near), (1, self.y_near, self.x_near)):
                src = near + 4 * shift
                wait = functools.partial(self.arrived, src, group, half)
                wait() if cond is None else pl.when(cond)(wait)
                self.forward(cond, src, group, half, target)

    def rest(self, group):
        for z in range(self.nz):
            up = 4 * (z - self.z)
            self.arrived(self.x_near + up, group, 1)
            self.arrived(self.y_near + up, group, 0)
            self.arrived(self.diagonal + up, group, 0)
            self.arrived(self.diagonal + up, group, 1)

    def drain(self):
        for cond, end in self.sends:
            end() if cond is None else pl.when(cond)(end)
        self.sends = []


def send_slots(n):
    nz = n // 4
    return 2 * 2 * (4 + 3 * 2 * (nz - 1) + 2 * nz)


def norm_rows(x, gains):
    average = jnp.mean(x, -1, keepdims=True)
    centred = x - average
    inverse = lax.rsqrt(jnp.mean(centred * centred, -1, keepdims=True) + epsilon)
    return centred, inverse, centred * inverse * gains


def norm_tangent(t, centred, inverse, gains):
    dcentred = t - jnp.mean(t, -1, keepdims=True)
    dinverse = -(inverse * inverse * inverse) * jnp.mean(centred * dcentred, -1, keepdims=True)
    return (dcentred * inverse + centred * dinverse) * gains


def softmax(scores):
    e = jnp.exp(scores - jnp.max(scores, -1, keepdims=True))
    return e / jnp.sum(e, -1, keepdims=True)


def first_layer(sizes, tokens, gain, a_full, b_full, normed, proj, att, state):
    micro, toks, width, hd, tangents = sizes
    for b in range(micro):
        x = tokens[b].astype(F32)
        normed[0, pl.ds(b * toks, toks), :] = norm_rows(x, gain[...])[2].astype(BF16)
    n = normed[0]
    for c in range(3 + tangents):
        at = pl.ds(c * hd, hd)
        proj[:, at] = dot(n, a_full[:, at]).astype(BF16)
    factor = HEAD ** (-0.5)
    even = lax.broadcasted_iota(jnp.int32, (toks, 2 * HEAD), 1) < HEAD
    even_v = lax.broadcasted_iota(jnp.int32, (toks, 2 * HEAD), 1) < HEAD
    for b in range(micro):
        rows = pl.ds(b * toks, toks)
        for pair in range(hd // (2 * HEAD)):
            lanes = pair * 2 * HEAD
            q = proj[rows, pl.ds(lanes, 2 * HEAD)]
            k = proj[rows, pl.ds(hd + lanes, 2 * HEAD)]
            vs = [proj[rows, pl.ds((2 + s) * hd + lanes, 2 * HEAD)] for s in range(1 + tangents)]
            zero = jnp.zeros_like(q)
            low = []
            for mine in (jnp.where(even, q, zero), jnp.where(even, zero, q)):
                low.append(softmax(dot_t(mine, k) * factor).astype(BF16))
            for s, v in enumerate(vs):
                joined = jnp.where(even_v, dot(low[0], v), dot(low[1], v))
                att[pl.ds(s * micro * toks + b * toks, toks), pl.ds(lanes, 2 * HEAD)] = joined.astype(BF16)
    rows0 = micro * toks
    tile = 256
    for c in range(width // tile):
        at = pl.ds(c * tile, tile)
        out = dot_t(att[...], b_full[0, at, :])
        extra = [dot_t(att[pl.ds(0, rows0), :], b_full[1 + j, at, :]) for j in range(tangents)]
        for b in range(micro):
            x = tokens[b, :, at].astype(F32)
            state[pl.ds(b * toks, toks), at] = (x + out[b * toks : (b + 1) * toks]).astype(BF16)
        for j in range(tangents):
            state[pl.ds((1 + j) * rows0, rows0), at] = (
                out[(1 + j) * rows0 : (2 + j) * rows0] + extra[j]
            ).astype(BF16)


def last_layer(sizes, gain, a_full, b_full, normed, state, classes):
    micro, toks, width, hd, tangents = sizes
    streams = 1 + tangents
    heads = hd // HEAD
    rows0 = micro * toks
    for b in range(micro):
        at = pl.ds(b * toks, toks)
        centred, inverse, y = norm_rows(state[at, :].astype(F32), gain[...])
        normed[0, at, :] = y.astype(BF16)
        for j in range(tangents):
            t = state[pl.ds((1 + j) * rows0 + b * toks, toks), :].astype(F32)
            normed[1 + j, at, :] = norm_tangent(t, centred, inverse, gain[...]).astype(BF16)
    block = 16
    firsts = [normed[s, pl.ds(b * toks, block), :] for b in range(micro) for s in range(streams)]
    q = dot(jnp.concatenate(firsts, 0), a_full[:, pl.ds(0, hd)])
    q = q.astype(BF16).astype(F32)
    mask = (
        lax.broadcasted_iota(jnp.int32, (heads, hd), 1) // HEAD
        == lax.broadcasted_iota(jnp.int32, (heads, hd), 0)
    ).astype(F32)
    spread = [q[i * block : i * block + 1] * mask for i in range(micro * streams)]
    u = dot_t(jnp.concatenate(spread, 0).astype(BF16), a_full[:, pl.ds(hd, hd)])
    factor = HEAD ** (-0.5)
    sums = []
    for b in range(micro):
        at = pl.ds(b * toks, toks)
        ub = u[b * streams * heads : (b + 1) * streams * heads]
        base = dot_t(ub.astype(BF16), normed[0, at, :]) * factor
        u0 = ub[:heads].astype(BF16)
        probs = softmax(base[:heads])
        weights = [probs]
        for j in range(tangents):
            ds = base[(1 + j) * heads : (2 + j) * heads] + dot_t(u0, normed[1 + j, at, :]) * factor
            weights.append(probs * (ds - jnp.sum(probs * ds, -1, keepdims=True)))
        m = dot(jnp.concatenate(weights, 0).astype(BF16), normed[0, at, :])
        low = probs.astype(BF16)
        parts = [m[:heads]]
        for j in range(tangents):
            parts.append(m[(1 + j) * heads : (2 + j) * heads] + dot(low, normed[1 + j, at, :]))
        sums += parts
    stacked = jnp.concatenate(sums, 0).astype(BF16)
    r = dot(stacked, a_full[:, pl.ds(2 * hd, hd)])
    zeros = jnp.concatenate([sums[b * streams] for b in range(micro)], 0).astype(BF16)
    extra = [dot(zeros, a_full[:, pl.ds((3 + j) * hd, hd)]) for j in range(tangents)]
    attended = []
    for s in range(streams):
        for b in range(micro):
            i = b * streams + s
            part = r[i * heads : (i + 1) * heads]
            if s > 0:
                part = part + extra[s - 1][b * heads : (b + 1) * heads]
            attended.append(jnp.sum(part * mask, 0, keepdims=True))
    total = classes.shape[0]
    attended.append(jnp.zeros((total - micro * streams, hd), F32))
    low = jnp.concatenate(attended, 0).astype(BF16)
    out = dot_t(low, b_full[0])
    more = [dot_t(low, b_full[1 + j])[:micro] for j in range(tangents)]
    filler = jnp.zeros((total - micro * streams, width), F32)
    out = out + jnp.concatenate([jnp.zeros((micro, width), F32)] + more + [filler], 0)
    resid = [
        state[pl.ds(s * rows0 + b * toks, 16), :].astype(F32)[:1] for s in range(streams) for b in range(micro)
    ]
    resid = jnp.concatenate(resid + [filler], 0)
    classes[...] = (resid + out).astype(BF16).astype(F32)


def kernel(
    n, sizes, tokens, w_qkv, tangent_value, outs, gain, final_gain, head, mean_ref, var_ref,
    a_full, b_full, normed, proj, att, state, state_in, classes, classes_in,
    send, recv, local, gate, core_sems,
):
    micro, toks, width, hd, tangents = sizes
    g = Gather(n, a_full, b_full, send, recv)
    me, section = g.me, g.section
    other = 1 - section
    up, down = g.z + 1 < g.nz, g.z >= 1

    barrier = pltpu.get_barrier_semaphore()

    def greet(target, sec):
        pl.semaphore_signal(
            barrier, inc=1, device_id={"section": sec, "dp": target}, device_id_type=MESH
        )

    greet(g.x_near, section)
    greet(g.y_near, section)
    greet(me, other)
    pl.when(up)(lambda: greet(me + 4, section))
    pl.when(down)(lambda: greet(me - 4, section))

    own = pl.ds(pl.multiple_of(me * g.rows, g.rows), g.rows)
    moves = [pltpu.make_async_copy(w_qkv, a_full.at[own, pl.ds(0, 3 * hd)], local.at[0])]
    for j in range(tangents):
        moves.append(
            pltpu.make_async_copy(
                tangent_value.at[j], a_full.at[own, pl.ds((3 + j) * hd, hd)], local.at[1 + j]
            )
        )
    moves.append(pltpu.make_async_copy(outs, b_full.at[:, own, :], local.at[1 + tangents]))
    for move in moves:
        move.start()
    for move in moves:
        move.wait()
    if g.nz > 1:
        middle = up & down
        pl.when(middle)(lambda: pl.semaphore_wait(barrier, 5))
        pl.when(jnp.logical_not(middle))(lambda: pl.semaphore_wait(barrier, 4))
    else:
        pl.semaphore_wait(barrier, 3)

    pl.when(section == 1)(lambda: pl.semaphore_wait(gate, 1))
    steps = [(group, d) for group in range(2) for d in range(g.nz)]
    g.direct(*steps[0])
    for i, step in enumerate(steps):
        if i + 1 < len(steps):
            g.direct(*steps[i + 1])
        g.relay(*step)
    g.rest(0)
    g.rest(1)
    g.drain()

    def across(src, dst, i):
        return pltpu.make_async_remote_copy(
            src_ref=src,
            dst_ref=dst,
            send_sem=core_sems.at[2 * i],
            recv_sem=core_sems.at[2 * i + 1],
            device_id={"section": other, "dp": me},
            device_id_type=MESH,
        )

    @pl.when(section == 0)
    def _():
        pl.semaphore_signal(
            gate, inc=1, device_id={"section": other, "dp": me}, device_id_type=MESH
        )
        first_layer(sizes, tokens, gain, a_full, b_full, normed, proj, att, state)
        onward = across(state, state_in, 0)
        onward.start()
        onward.wait_send()
        across(classes, classes_in, 1).wait_recv()

    @pl.when(section == 1)
    def _():
        across(state, state_in, 0).wait_recv()
        last_layer(sizes, gain, a_full, b_full, normed, state_in, classes)
        back = across(classes, classes_in, 1)
        back.start()
        classes_in[...] = classes[...]
        back.wait_send()

    rows = classes_in[...]
    count = classes_in.shape[0]
    primal = jnp.concatenate([rows[:micro]] * (1 + tangents) + [rows[(1 + tangents) * micro :]], 0)
    centred, inverse, y = norm_rows(primal, final_gain[...])
    dy = norm_tangent(rows, centred, inverse, final_gain[...])
    which = lax.broadcasted_iota(jnp.int32, (count, width), 0)
    logits = dot(jnp.where(which < micro, y, dy).astype(BF16), head[...])
    mean_ref[...] = logits[:micro]
    var_ref[...] = sum(
        logits[(1 + j) * micro : (2 + j) * micro] * logits[(1 + j) * micro : (2 + j) * micro]
        for j in range(tangents)
    )


def two_sections(n):
    def shards(tokens, w_qkv, w_output, tangent_value, tangent_output, layer_gain, final_gain, head):
        micro, _, toks, width = tokens.shape
        tangents = tangent_value.shape[1]
        hd = w_output.shape[1]
        classes = head.shape[1]
        rows = width // n
        outs = jnp.swapaxes(jnp.concatenate([w_output, tangent_output[0]], 0), 1, 2)
        sizes = (micro, toks, width, hd, tangents)
        vmem = pl.BlockSpec(memory_space=pltpu.VMEM)
        anywhere = pl.BlockSpec(memory_space=pl.ANY)
        streams = 1 + tangents
        padded = -(-micro * streams // 8) * 8
        all_rows = streams * micro * toks
        mean, var = pl.pallas_call(
            functools.partial(kernel, n, sizes),
            out_shape=[jax.ShapeDtypeStruct((micro, classes), F32)] * 2,
            in_specs=[vmem, anywhere, anywhere, anywhere, vmem, vmem, vmem],
            out_specs=[vmem, vmem],
            scratch_shapes=[
                pltpu.VMEM((width, (3 + tangents) * hd), BF16),
                pltpu.VMEM((streams, width, hd), BF16),
                pltpu.VMEM((streams, micro * toks, width), BF16),
                pltpu.VMEM((micro * toks, (3 + tangents) * hd), BF16),
                pltpu.VMEM((all_rows, hd), BF16),
                pltpu.VMEM((all_rows, width), BF16),
                pltpu.VMEM((all_rows, width), BF16),
                pltpu.VMEM((padded, width), F32),
                pltpu.VMEM((padded, width), F32),
                pltpu.SemaphoreType.DMA((send_slots(n),)),
                pltpu.SemaphoreType.DMA((n, 4)),
                pltpu.SemaphoreType.DMA((2 + tangents,)),
                pltpu.SemaphoreType.REGULAR,
                pltpu.SemaphoreType.DMA((4,)),
            ],
            compiler_params=pltpu.CompilerParams(
                collective_id=0, has_side_effects=True, vmem_limit_bytes=60 * 2**20
            ),
        )(
            tokens.reshape(micro, toks, width),
            w_qkv[0],
            tangent_value[0],
            outs,
            layer_gain,
            final_gain[None],
            head,
        )
        return mean[:, None, :], var[:, None, :]

    return shards


def solution(mesh):
    n = mesh.shape["dp"]
    fast = mesh.shape["section"] == 2 and n % 4 == 0
    return jax.shard_map(
        two_sections(n) if fast else relay_shards,
        mesh=mesh,
        in_specs=(
            P(None, "dp", None, None),
            P("section", "dp", None),
            P("section", None, "dp"),
            P("section", None, "dp", None),
            P("section", None, None, "dp"),
            P("section", None),
            P(),
            P(None, "section"),
        ),
        out_specs=(P(None, "dp", "section"), P(None, "dp", "section")),
        check_vma=False,
    )
```

time: 364 us -> 94.4 us (0.26)
  waiting for transfers between devices: 247 us -> 0 us
  Pallas kernels: 0 us -> 87.7 us
  blocking collectives: 41.8 us -> 0 us
  local copies, waits for them, and re-layouts: 36.2 us -> 4.22 us
  matrix products: 15.6 us -> 0 us
  between operations: 13.8 us -> 0.65 us
  other arithmetic: 6.18 us -> 1.61 us
    all_gather x4 -> x0, waiting for transfers between devices: 240 us -> none  [the longest x1 69.3 us: shards(): lax.all_gather(w_qkv, 'dp', axis=1, tiled=True)]
    pallas_call x0 -> x1, Pallas kernels: none -> 87.7 us  [shards(): pl.pallas_call(functools.partial(kernel, n, sizes), out_shape=[jax.ShapeD...]
    psum x1 -> x0, blocking collectives: 41.8 us -> none  [spread(): return lax.psum(jnp.where(mine, shard, jnp.zeros_like(shard)), axis)]
    dot_general x10 -> x0, matrix products: 13.3 us -> none  [contract(): return jnp.einsum(spec, left, right, preferred_element_type=jnp.float32)]
    while x3 -> x0, local copies, waits for them, and re-layouts: 10.5 us -> none  [shards(): lax.fori_loop(0, section_count, advance, jnp.zeros_like(entering))]
    slice x7 -> x0, local copies, waits for them, and re-layouts: 8.71 us -> none  [the longest x2 4.16 us: layer_step(): key_rows[1:]]
    another operation x4 -> x0, local copies, waits for them, and re-layouts: 4.96 us -> none
    ppermute x2 -> x0, waiting for transfers between devices: 4.63 us -> none  [passed_along(): return lax.ppermute(block, axis, route)]
  transfers between devices with their start and end apart: 6 -> 0, of which waited for: 6 -> 0; matrix products, arithmetic and copies ran while one was open for 3% -> 0% of each run, Pallas kernels for 0% -> 0%
where the time goes in v1:
time: 94.4 us; the launch traced here: 94.2 us
  Pallas kernels  87.7 us (93%)
  local copies, waits for them, and re-layouts  4.22 us (4%)
  other arithmetic  1.61 us (2%)
    pallas_call x1, Pallas kernels, shards(): pl.pallas_call(functools.partial(kernel, n, sizes), out_shape=[jax.ShapeD...  87.7 us
    unnamed x7, local copies, waits for them, and re-layouts  4.22 us

profile of v1, /device:TPU:0, one launch (start us, length us, event | category | flops | bytes accessed | tf_op | source)
XLA Modules:
  0.0 94.2 jit_solution(10449623752679608353)
XLA Ops:
  0.6 1.6 %maximum_bitcast_fusion.outs = bf16[3,64,512]{2,1,0:T(8,128)(2,1)} fusion(bf16[2,512,64]{1,2,0:T(8,128)(2,1)} %bitcast.11, bf16[1,512,64]{1,2,0:T(8,128)(2,1)} %param.10), kind=kLoop, calls=%fused_computation | loop fusion | flops 98304 | bytes 393216 | tf_op jit(solution)/shard_map/transpose | solution.py:443
  2.2 2.3 %copy.10.head = bf16[1024,500]{1,0:T(8,128)(2,1)} copy(bf16[1024,500]{0,1:T(8,128)(2,1)} %param.15) | data formatting | bytes 2048000 | tf_op args[7]
  4.5 87.7 %shard_map.95 = (f32[2,500]{1,0:T(2,128)}, f32[2,500]{1,0:T(2,128)}) custom-call(bf16[2,80,1024]{2,1,0:T(8,128)(2,1)} %bitcast.9, bf16[64,1536]{1,0:T(8,128)(2,1)} %bitcast.10, bf16[2,64,512]{2,1,0:T(8,128)(2,1)} %bitcast.12, bf16[3,64,512]{2,1,0:T(8,128)(2,1)} %maximum_bitcast_fusion.outs, f32[1,1024]{1,0:T(1,128)} %gain.1, f32[1,1024]{1,0:T(1,128)} %bitcast.13, ...), custom_call_target="tpu_custom_call" | custom-call | tf_op jit(solution)/shard_map/pallas_call | solution.py:450
  92.2 0.0 copy-start.1
  92.2 0.7 copy-done.1
  92.9 0.0 copy-start
  92.9 0.6 copy.11
  93.5 0.1 copy-done
  93.6 0.6 copy.12
Async XLA Ops:
  92.2 0.7 copy-start.1
  92.9 0.7 copy-start

commit v2 on v1

--- a/solution.py
+++ b/solution.py
@@ -227,32 +227,43 @@
     return e / jnp.sum(e, -1, keepdims=True)
 
 
-def first_layer(sizes, tokens, gain, a_full, b_full, normed, proj, att, state):
+def first_norm(sizes, tokens, gain, normed):
     micro, toks, width, hd, tangents = sizes
     for b in range(micro):
         x = tokens[b].astype(F32)
         normed[0, pl.ds(b * toks, toks), :] = norm_rows(x, gain[...])[2].astype(BF16)
+
+
+def first_qkv(sizes, a_full, normed, proj):
+    micro, toks, width, hd, tangents = sizes
     n = normed[0]
     for c in range(3 + tangents):
         at = pl.ds(c * hd, hd)
         proj[:, at] = dot(n, a_full[:, at]).astype(BF16)
+
+
+def first_attend(sizes, proj, att, b):
+    micro, toks, width, hd, tangents = sizes
     factor = HEAD ** (-0.5)
     even = lax.broadcasted_iota(jnp.int32, (toks, 2 * HEAD), 1) < HEAD
-    even_v = lax.broadcasted_iota(jnp.int32, (toks, 2 * HEAD), 1) < HEAD
-    for b in range(micro):
-        rows = pl.ds(b * toks, toks)
-        for pair in range(hd // (2 * HEAD)):
-            lanes = pair * 2 * HEAD
-            q = proj[rows, pl.ds(lanes, 2 * HEAD)]
-            k = proj[rows, pl.ds(hd + lanes, 2 * HEAD)]
-            vs = [proj[rows, pl.ds((2 + s) * hd + lanes, 2 * HEAD)] for s in range(1 + tangents)]
-            zero = jnp.zeros_like(q)
-            low = []
-            for mine in (jnp.where(even, q, zero), jnp.where(even, zero, q)):
-                low.append(softmax(dot_t(mine, k) * factor).astype(BF16))
-            for s, v in enumerate(vs):
-                joined = jnp.where(even_v, dot(low[0], v), dot(low[1], v))
-                att[pl.ds(s * micro * toks + b * toks, toks), pl.ds(lanes, 2 * HEAD)] = joined.astype(BF16)
+    rows = pl.ds(b * toks, toks)
+    for pair in range(hd // (2 * HEAD)):
+        lanes = pair * 2 * HEAD
+        q = proj[rows, pl.ds(lanes, 2 * HEAD)]
+        k = proj[rows, pl.ds(hd + lanes, 2 * HEAD)]
+        vs = [proj[rows, pl.ds((2 + s) * hd + lanes, 2 * HEAD)] for s in range(1 + tangents)]
+        zero = jnp.zeros_like(q)
+        low = []
+        for mine in (jnp.where(even, q, zero), jnp.where(even, zero, q)):
+            low.append(softmax(dot_t(mine, k) * factor).astype(BF16))
+        for s, v in enumerate(vs):
+            joined = jnp.where(even, dot(low[0], v), dot(low[1], v))
+            at = pl.ds((s * micro + b) * toks, toks)
+            att[at, pl.ds(lanes, 2 * HEAD)] = joined.astype(BF16)
+
+
+def first_out(sizes, tokens, b_full, att, state):
+    micro, toks, width, hd, tangents = sizes
     rows0 = micro * toks
     tile = 256
     for c in range(width // tile):
@@ -268,10 +279,105 @@
             ).astype(BF16)
 
 
-def last_layer(sizes, gain, a_full, b_full, normed, state, classes):
+BLOCK = 16
+
+
+class Plane:
+    def __init__(self, g, send, recv):
+        self.g, self.send, self.recv = g, send, recv
+        self.place = g.me % 4
+        self.peers = (g.diagonal, g.x_near, g.y_near)
+
+    def copy(self, stage, i, src, dst, source):
+        return pltpu.make_async_remote_copy(
+            src_ref=src,
+            dst_ref=dst,
+            send_sem=self.send.at[stage, i],
+            recv_sem=self.recv.at[stage, source],
+            device_id={"section": self.g.section, "dp": self.peers[i]},
+            device_id_type=MESH,
+        )
+
+    def exchange(self, stage, out_of, into):
+        for i, peer in enumerate(self.peers):
+            self.copy(stage, i, out_of(peer % 4), into(self.place), self.place).start()
+
+    def arrive(self, stage, out_of, into):
+        for i, peer in enumerate(self.peers):
+            self.copy(stage, i, out_of(peer % 4), into(peer % 4), peer % 4).wait_recv()
+
+    def finish(self, stage, out_of, into):
+        for i, peer in enumerate(self.peers):
+            self.copy(stage, i, out_of(peer % 4), into(self.place), self.place).wait_send()
+
+
+class Line:
+    def __init__(self, g, parts, send, recv):
+        self.g, self.parts, self.send, self.recv = g, parts, send, recv
+        self.sends = []
+
+    def copy(self, z, group, way, target):
+        rows = 4 * self.g.rows
+        at = pl.ds(pl.multiple_of(z * rows, rows), rows)
+        ref = self.parts[0].at[at, :] if group == 0 else self.parts[1].at[:, at, :]
+        return pltpu.make_async_remote_copy(
+            src_ref=ref,
+            dst_ref=ref,
+            send_sem=self.send.at[z, 2 * group + way],
+            recv_sem=self.recv.at[z, group],
+            device_id={"section": self.g.section, "dp": target},
+            device_id_type=MESH,
+        )
+
+    def run(self, group):
+        g = self.g
+        for d in range(g.nz):
+            for shift, cond in g.sources(d):
+                z = g.z + shift
+
+                def step(z=z, shift=shift, d=d):
+                    if d > 0:
+                        self.copy(z, group, 0, g.me).wait_recv()
+                    if shift <= 0 and d < g.nz - 1:
+                        pl.when(g.z + 1 < g.nz)(lambda: self.copy(z, group, 0, g.me + 4).start())
+                    if shift >= 0 and d < g.nz - 1:
+                        pl.when(g.z >= 1)(lambda: self.copy(z, group, 1, g.me - 4).start())
+
+                step() if cond is None else pl.when(cond)(step)
+
+    def drain(self, group):
+        g = self.g
+        for d in range(g.nz - 1):
+            for shift, cond in g.sources(d):
+                z = g.z + shift
+
+                def step(z=z, shift=shift):
+                    if shift <= 0:
+                        pl.when(g.z + 1 < g.nz)(lambda: self.copy(z, group, 0, g.me + 4).wait_send())
+                    if shift >= 0:
+                        pl.when(g.z >= 1)(lambda: self.copy(z, group, 1, g.me - 4).wait_send())
+
+                step() if cond is None else pl.when(cond)(step)
+
+
+def class_rows(sizes, gain, state):
     micro, toks, width, hd, tangents = sizes
     streams = 1 + tangents
-    heads = hd // HEAD
+    rows0 = micro * toks
+    filler = [jnp.zeros((BLOCK - micro * streams, width), F32)]
+    heads_of = [
+        state[pl.ds(s * rows0 + b * toks, 16), :].astype(F32)[:1] for s in range(streams) for b in range(micro)
+    ]
+    resid = jnp.concatenate(heads_of + filler, 0)
+    primal = jnp.concatenate(heads_of[:micro] * streams + filler, 0)
+    centred, inverse, y = norm_rows(primal, gain[...])
+    dy = norm_tangent(resid, centred, inverse, gain[...])
+    which = lax.broadcasted_iota(jnp.int32, resid.shape, 0)
+    return resid, jnp.where(which < micro, y, dy).astype(BF16)
+
+
+def last_norm(sizes, gain, state, normed):
+    micro, toks, width, hd, tangents = sizes
     rows0 = micro * toks
     for b in range(micro):
         at = pl.ds(b * toks, toks)
@@ -280,23 +386,18 @@
         for j in range(tangents):
             t = state[pl.ds((1 + j) * rows0 + b * toks, toks), :].astype(F32)
             normed[1 + j, at, :] = norm_tangent(t, centred, inverse, gain[...]).astype(BF16)
-    block = 16
-    firsts = [normed[s, pl.ds(b * toks, block), :] for b in range(micro) for s in range(streams)]
-    q = dot(jnp.concatenate(firsts, 0), a_full[:, pl.ds(0, hd)])
-    q = q.astype(BF16).astype(F32)
-    mask = (
-        lax.broadcasted_iota(jnp.int32, (heads, hd), 1) // HEAD
-        == lax.broadcasted_iota(jnp.int32, (heads, hd), 0)
-    ).astype(F32)
-    spread = [q[i * block : i * block + 1] * mask for i in range(micro * streams)]
-    u = dot_t(jnp.concatenate(spread, 0).astype(BF16), a_full[:, pl.ds(hd, hd)])
+
+
+def last_attend(sizes, heads, u, normed):
+    micro, toks, width, hd, tangents = sizes
+    streams = 1 + tangents
     factor = HEAD ** (-0.5)
     sums = []
     for b in range(micro):
         at = pl.ds(b * toks, toks)
-        ub = u[b * streams * heads : (b + 1) * streams * heads]
-        base = dot_t(ub.astype(BF16), normed[0, at, :]) * factor
-        u0 = ub[:heads].astype(BF16)
+        ub = u[b * streams * heads : (b + 1) * streams * heads].astype(BF16)
+        base = dot_t(ub, normed[0, at, :]) * factor
+        u0 = ub[:heads]
         probs = softmax(base[:heads])
         weights = [probs]
         for j in range(tangents):
@@ -308,42 +409,46 @@
         for j in range(tangents):
             parts.append(m[(1 + j) * heads : (2 + j) * heads] + dot(low, normed[1 + j, at, :]))
         sums += parts
-    stacked = jnp.concatenate(sums, 0).astype(BF16)
-    r = dot(stacked, a_full[:, pl.ds(2 * hd, hd)])
-    zeros = jnp.concatenate([sums[b * streams] for b in range(micro)], 0).astype(BF16)
-    extra = [dot(zeros, a_full[:, pl.ds((3 + j) * hd, hd)]) for j in range(tangents)]
-    attended = []
-    for s in range(streams):
-        for b in range(micro):
-            i = b * streams + s
-            part = r[i * heads : (i + 1) * heads]
-            if s > 0:
-                part = part + extra[s - 1][b * heads : (b + 1) * heads]
-            attended.append(jnp.sum(part * mask, 0, keepdims=True))
-    total = classes.shape[0]
-    attended.append(jnp.zeros((total - micro * streams, hd), F32))
-    low = jnp.concatenate(attended, 0).astype(BF16)
-    out = dot_t(low, b_full[0])
-    more = [dot_t(low, b_full[1 + j])[:micro] for j in range(tangents)]
-    filler = jnp.zeros((total - micro * streams, width), F32)
-    out = out + jnp.concatenate([jnp.zeros((micro, width), F32)] + more + [filler], 0)
-    resid = [
-        state[pl.ds(s * rows0 + b * toks, 16), :].astype(F32)[:1] for s in range(streams) for b in range(micro)
-    ]
-    resid = jnp.concatenate(resid + [filler], 0)
-    classes[...] = (resid + out).astype(BF16).astype(F32)
+    return jnp.concatenate(sums, 0).astype(BF16)
+
+
+def order(sizes, heads, flip):
+    micro, toks, width, hd, tangents = sizes
+    streams = 1 + tangents
+    share = heads // 4
+    few, many = micro * streams * heads, heads * BLOCK
+    shape = (many, few) if flip else (few, many)
+    r = lax.broadcasted_iota(jnp.int32, shape, 1 if flip else 0)
+    c = lax.broadcasted_iota(jnp.int32, shape, 0 if flip else 1)
+    head, i = r % heads, r // heads
+    i = (i % streams) * micro + i // streams
+    return (c == head * BLOCK + i).astype(F32).astype(BF16)
+
+
+def lowered(extra, micro, rows):
+    width = extra[0].shape[-1]
+    parts = [jnp.zeros((micro, width), F32)] + [e[:micro] for e in extra]
+    used = micro * len(parts)
+    return jnp.concatenate(parts + [jnp.zeros((rows - used, width), F32)], 0)
 
 
 def kernel(
     n, sizes, tokens, w_qkv, tangent_value, outs, gain, final_gain, head, mean_ref, var_ref,
     a_full, b_full, normed, proj, att, state, state_in, classes, classes_in,
-    send, recv, local, gate, core_sems,
+    a_quarter, b_quarter, a_part, b_part, cls_all, u_out, u_all, m_out, m_all, o_out, o_all,
+    send, recv, local, gate, core_sems, plane_send, plane_recv, line_send, line_recv,
 ):
     micro, toks, width, hd, tangents = sizes
+    streams = 1 + tangents
+    heads = hd // HEAD
+    share = heads // 4
+    part = share * HEAD
     g = Gather(n, a_full, b_full, send, recv)
     me, section = g.me, g.section
     other = 1 - section
     up, down = g.z + 1 < g.nz, g.z >= 1
+    plane = Plane(g, plane_send, plane_recv)
+    line = Line(g, (a_part, b_part), line_send, line_recv)
 
     barrier = pltpu.get_barrier_semaphore()
 
@@ -352,42 +457,19 @@
             barrier, inc=1, device_id={"section": sec, "dp": target}, device_id_type=MESH
         )
 
-    greet(g.x_near, section)
-    greet(g.y_near, section)
+    for near in (g.x_near, g.y_near, g.diagonal):
+        greet(near, section)
     greet(me, other)
     pl.when(up)(lambda: greet(me + 4, section))
     pl.when(down)(lambda: greet(me - 4, section))
 
-    own = pl.ds(pl.multiple_of(me * g.rows, g.rows), g.rows)
-    moves = [pltpu.make_async_copy(w_qkv, a_full.at[own, pl.ds(0, 3 * hd)], local.at[0])]
-    for j in range(tangents):
-        moves.append(
-            pltpu.make_async_copy(
-                tangent_value.at[j], a_full.at[own, pl.ds((3 + j) * hd, hd)], local.at[1 + j]
-            )
-        )
-    moves.append(pltpu.make_async_copy(outs, b_full.at[:, own, :], local.at[1 + tangents]))
-    for move in moves:
-        move.start()
-    for move in moves:
-        move.wait()
-    if g.nz > 1:
-        middle = up & down
-        pl.when(middle)(lambda: pl.semaphore_wait(barrier, 5))
-        pl.when(jnp.logical_not(middle))(lambda: pl.semaphore_wait(barrier, 4))
-    else:
-        pl.semaphore_wait(barrier, 3)
-
-    pl.when(section == 1)(lambda: pl.semaphore_wait(gate, 1))
-    steps = [(group, d) for group in range(2) for d in range(g.nz)]
-    g.direct(*steps[0])
-    for i, step in enumerate(steps):
-        if i + 1 < len(steps):
-            g.direct(*steps[i + 1])
-        g.relay(*step)
-    g.rest(0)
-    g.rest(1)
-    g.drain()
+    def met():
+        if g.nz > 1:
+            middle = up & down
+            pl.when(middle)(lambda: pl.semaphore_wait(barrier, 6))
+            pl.when(jnp.logical_not(middle))(lambda: pl.semaphore_wait(barrier, 5))
+        else:
+            pl.semaphore_wait(barrier, 4)
 
     def across(src, dst, i):
         return pltpu.make_async_remote_copy(
@@ -399,24 +481,159 @@
             device_id_type=MESH,
         )
 
+    own = pl.ds(pl.multiple_of(me * g.rows, g.rows), g.rows)
+
+    def moved(pairs):
+        moves = [pltpu.make_async_copy(src, dst, local.at[i]) for i, (src, dst) in enumerate(pairs)]
+        for move in moves:
+            move.start()
+        for move in moves:
+            move.wait()
+
+    met()
+
     @pl.when(section == 0)
     def _():
-        pl.semaphore_signal(
-            gate, inc=1, device_id={"section": other, "dp": me}, device_id_type=MESH
-        )
-        first_layer(sizes, tokens, gain, a_full, b_full, normed, proj, att, state)
+        pairs = [(w_qkv, a_full.at[own, pl.ds(0, 3 * hd)])]
+        for j in range(tangents):
+            pairs.append((tangent_value.at[j], a_full.at[own, pl.ds((3 + j) * hd, hd)]))
+        pairs.append((outs, b_full.at[:, own, :]))
+        moved(pairs)
+        steps = [(group, d) for group in range(2) for d in range(g.nz)]
+        g.direct(*steps[0])
+        first_norm(sizes, tokens, gain, normed)
+        for i, step in enumerate(steps):
+            if step == (1, 0):
+                g.rest(0)
+                first_qkv(sizes, a_full, normed, proj)
+            if step[0] == 1 and 1 <= step[1] <= micro:
+                first_attend(sizes, proj, att, step[1] - 1)
+            if i + 1 < len(steps):
+                g.direct(*steps[i + 1])
+            if i + 1 == g.nz + min(1, g.nz - 1):
+                pl.semaphore_signal(
+                    gate, inc=1, device_id={"section": other, "dp": me}, device_id_type=MESH
+                )
+            g.relay(*step)
+        for b in range(g.nz - 1, micro):
+            first_attend(sizes, proj, att, b)
+        g.rest(1)
+        first_out(sizes, tokens, b_full, att, state)
         onward = across(state, state_in, 0)
         onward.start()
+        g.drain()
         onward.wait_send()
         across(classes, classes_in, 1).wait_recv()
 
     @pl.when(section == 1)
     def _():
+        pairs = []
+        for p in range(4):
+            for m in range(3):
+                pairs.append(
+                    (w_qkv.at[:, pl.ds(m * hd + p * part, part)], a_quarter.at[p, :, pl.ds(m * part, part)])
+                )
+            for j in range(tangents):
+                pairs.append(
+                    (
+                        tangent_value.at[j, :, pl.ds(p * part, part)],
+                        a_quarter.at[p, :, pl.ds((3 + j) * part, part)],
+                    )
+                )
+            pairs.append((outs.at[:, :, pl.ds(p * part, part)], b_quarter.at[p]))
+        moved(pairs)
+
+        def at_place(place):
+            row = (g.z * 4 + place) * g.rows
+            return pl.ds(pl.multiple_of(row, g.rows), g.rows)
+
+        stages = [
+            (0, lambda p: a_quarter.at[p], lambda p: a_part.at[at_place(p), :]),
+            (1, lambda p: b_quarter.at[p], lambda p: b_part.at[:, at_place(p), :]),
+            (2, lambda p: cls_all.at[plane.place], lambda p: cls_all.at[p]),
+            (3, lambda p: u_out.at[p], lambda p: u_all.at[p]),
+            (4, lambda p: m_out.at[p], lambda p: m_all.at[p]),
+            (5, lambda p: o_out.at[p], lambda p: o_all.at[p]),
+        ]
+        for stage in stages[:2]:
+            plane.exchange(*stage)
+        moved(
+            [
+                (a_quarter.at[plane.place], a_part.at[own, :]),
+                (b_quarter.at[plane.place], b_part.at[:, own, :]),
+            ]
+        )
+        for stage in stages[:2]:
+            plane.arrive(*stage)
+        pl.semaphore_wait(gate, 1)
+        line.run(0)
+        line.run(1)
+
         across(state, state_in, 0).wait_recv()
-        last_layer(sizes, gain, a_full, b_full, normed, state_in, classes)
+        resid, firsts = class_rows(sizes, gain, state_in)
+        cls_all[plane.place] = firsts
+        plane.exchange(*stages[2])
+        last_norm(sizes, gain, state_in, normed)
+        plane.arrive(*stages[2])
+        rows = jnp.concatenate([cls_all[k] for k in range(4)], 0)
+        q = dot(rows, a_part[:, pl.ds(0, part)]).astype(BF16)
+        owner = lax.broadcasted_iota(jnp.int32, (BLOCK, part), 1) // HEAD
+        zero = jnp.zeros((BLOCK, part), F32)
+        spread = []
+        for k in range(4):
+            block = q[k * BLOCK : (k + 1) * BLOCK].astype(F32)
+            spread += [jnp.where(owner == h, block, zero) for h in range(share)]
+        u = dot_t(jnp.concatenate(spread, 0).astype(BF16), a_part[:, pl.ds(part, part)]).astype(BF16)
+        tall = share * BLOCK
+        for k in range(4):
+            u_out[k] = u[k * tall : (k + 1) * tall]
+        plane.exchange(*stages[3])
+        u_all[plane.place] = u_out[plane.place]
+        plane.arrive(*stages[3])
+        u48 = dot(order(sizes, heads, False), jnp.concatenate([u_all[k] for k in range(4)], 0))
+        sums = last_attend(sizes, heads, u48, normed)
+        spreadm = dot(order(sizes, heads, True), sums).astype(BF16)
+        for k in range(4):
+            m_out[k] = spreadm[k * tall : (k + 1) * tall]
+        plane.exchange(*stages[4])
+        m_all[plane.place] = m_out[plane.place]
+        plane.arrive(*stages[4])
+        m = jnp.concatenate([m_all[k] for k in range(4)], 0)
+        r = [dot(m, a_part[:, pl.ds((2 + c) * part, part)]) for c in range(streams)]
+
+        def picked(x, k):
+            chosen = zero
+            for h in range(share):
+                at = k * tall + h * BLOCK
+                chosen = jnp.where(owner == h, x[at : at + BLOCK], chosen)
+            return chosen
+
+        attended = jnp.concatenate(
+            [
+                picked(r[0], k) + lowered([picked(x, k) for x in r[1:]], micro, BLOCK)
+                for k in range(4)
+            ],
+            0,
+        ).astype(BF16)
+        out = [dot_t(attended, b_part[c]) for c in range(streams)]
+        some = o_out.shape[1]
+        for k in range(4):
+            at = k * BLOCK
+            extra = [x[at : at + micro] for x in out[1:]]
+            o_out[k] = out[0][at : at + some] + lowered(extra, micro, some)
+        plane.exchange(*stages[5])
+        o_all[plane.place] = o_out[plane.place]
+        plane.arrive(*stages[5])
+        total = o_all[0] + o_all[1] + o_all[2] + o_all[3]
+        final = (resid[:some] + total).astype(BF16).astype(F32)
+        classes[...] = final
         back = across(classes, classes_in, 1)
         back.start()
-        classes_in[...] = classes[...]
+        classes_in[...] = final
+        for stage in stages:
+            plane.finish(*stage)
+        line.drain(0)
+        line.drain(1)
         back.wait_send()
 
     rows = classes_in[...]
@@ -425,7 +642,7 @@
     centred, inverse, y = norm_rows(primal, final_gain[...])
     dy = norm_tangent(rows, centred, inverse, final_gain[...])
     which = lax.broadcasted_iota(jnp.int32, (count, width), 0)
-    logits = dot(jnp.where(which < micro, y, dy).astype(BF16), head[...])
+    logits = dot_t(jnp.where(which < micro, y, dy).astype(BF16), head[...])
     mean_ref[...] = logits[:micro]
     var_ref[...] = sum(
         logits[(1 + j) * micro : (2 + j) * micro] * logits[(1 + j) * micro : (2 + j) * micro]
@@ -447,6 +664,7 @@
         streams = 1 + tangents
         padded = -(-micro * streams // 8) * 8
         all_rows = streams * micro * toks
+        tall = hd // HEAD // 4 * BLOCK
         mean, var = pl.pallas_call(
             functools.partial(kernel, n, sizes),
             out_shape=[jax.ShapeDtypeStruct((micro, classes), F32)] * 2,
@@ -462,11 +680,26 @@
                 pltpu.VMEM((all_rows, width), BF16),
                 pltpu.VMEM((padded, width), F32),
                 pltpu.VMEM((padded, width), F32),
+                pltpu.VMEM((4, rows, (3 + tangents) * hd // 4), BF16),
+                pltpu.VMEM((4, streams, rows, hd // 4), BF16),
+                pltpu.VMEM((width, (3 + tangents) * hd // 4), BF16),
+                pltpu.VMEM((streams, width, hd // 4), BF16),
+                pltpu.VMEM((4, BLOCK, width), BF16),
+                pltpu.VMEM((4, tall, width), BF16),
+                pltpu.VMEM((4, tall, width), BF16),
+                pltpu.VMEM((4, tall, width), BF16),
+                pltpu.VMEM((4, tall, width), BF16),
+                pltpu.VMEM((4, padded, width), F32),
+                pltpu.VMEM((4, padded, width), F32),
                 pltpu.SemaphoreType.DMA((send_slots(n),)),
                 pltpu.SemaphoreType.DMA((n, 4)),
-                pltpu.SemaphoreType.DMA((2 + tangents,)),
+                pltpu.SemaphoreType.DMA((4 * (4 + tangents),)),
                 pltpu.SemaphoreType.REGULAR,
                 pltpu.SemaphoreType.DMA((4,)),
+                pltpu.SemaphoreType.DMA((6, 3)),
+                pltpu.SemaphoreType.DMA((6, 4)),
+                pltpu.SemaphoreType.DMA((n // 4, 4)),
+                pltpu.SemaphoreType.DMA((n // 4, 2)),
             ],
             compiler_params=pltpu.CompilerParams(
                 collective_id=0, has_side_effects=True, vmem_limit_bytes=60 * 2**20
@@ -478,7 +711,7 @@
             outs,
             layer_gain,
             final_gain[None],
-            head,
+            head.T,
         )
         return mean[:, None, :], var[:, None, :]
 

time: 94.4 us -> 85.7 us (0.908)
  Pallas kernels: 87.7 us -> 81.3 us
  local copies, waits for them, and re-layouts: 4.22 us -> 1.94 us
    pallas_call x1, Pallas kernels: 87.7 us -> 81.3 us  [shards(): pl.pallas_call(functools.partial(kernel, n, sizes), out_shape=[jax.ShapeD...]
    unnamed x7 -> x6, local copies, waits for them, and re-layouts: 4.22 us -> 1.94 us
where the time goes in v2:
time: 85.7 us; the launch traced here: 85.5 us
  Pallas kernels  81.3 us (95%)
  local copies, waits for them, and re-layouts  1.94 us (2%)
  other arithmetic  1.59 us (2%)
    pallas_call x1, Pallas kernels, shards(): pl.pallas_call(functools.partial(kernel, n, sizes), out_shape=[jax.ShapeD...  81.3 us
    unnamed x6, local copies, waits for them, and re-layouts  1.94 us

profile of v2, /device:TPU:0, one launch (start us, length us, event | category | flops | bytes accessed | tf_op | source)
XLA Modules:
  0.0 85.5 jit_solution(833599854116180918)
XLA Ops:
  0.6 1.6 %maximum_bitcast_fusion.outs = bf16[3,64,512]{2,1,0:T(8,128)(2,1)} fusion(bf16[2,512,64]{1,2,0:T(8,128)(2,1)} %bitcast.13, bf16[1,512,64]{1,2,0:T(8,128)(2,1)} %param.10), kind=kLoop, calls=%fused_computation | loop fusion | flops 98304 | bytes 393216 | tf_op jit(solution)/shard_map/transpose | solution.py:660
  2.2 81.3 %shard_map.95 = (f32[2,500]{1,0:T(2,128)}, f32[2,500]{1,0:T(2,128)}) custom-call(bf16[2,80,1024]{2,1,0:T(8,128)(2,1)} %bitcast.11, bf16[64,1536]{1,0:T(8,128)(2,1)} %bitcast.12, bf16[2,64,512]{2,1,0:T(8,128)(2,1)} %bitcast.14, bf16[3,64,512]{2,1,0:T(8,128)(2,1)} %maximum_bitcast_fusion.outs, f32[1,1024]{1,0:T(1,128)} %gain.1, f32[1,1024]{1,0:T(1,128)} %bitcast.17, ...), custom_call_target="tpu_custom_call" | custom-call | tf_op jit(solution)/shard_map/pallas_call | solution.py:668
  83.5 0.0 copy-start.1
  83.5 0.7 copy-done.1
  84.2 0.0 copy-start
  84.2 0.6 copy.10
  84.8 0.1 copy-done
  84.9 0.6 copy.11
Async XLA Ops:
  83.5 0.7 copy-start.1
  84.2 0.7 copy-start

commit v3 on v2

--- a/solution.py
+++ b/solution.py
@@ -500,23 +500,26 @@
         pairs.append((outs, b_full.at[:, own, :]))
         moved(pairs)
         steps = [(group, d) for group in range(2) for d in range(g.nz)]
-        g.direct(*steps[0])
-        first_norm(sizes, tokens, gain, normed)
-        for i, step in enumerate(steps):
-            if step == (1, 0):
-                g.rest(0)
-                first_qkv(sizes, a_full, normed, proj)
-            if step[0] == 1 and 1 <= step[1] <= micro:
-                first_attend(sizes, proj, att, step[1] - 1)
-            if i + 1 < len(steps):
-                g.direct(*steps[i + 1])
-            if i + 1 == g.nz + min(1, g.nz - 1):
+        lag = 2
+        chunks = [
+            lambda: (g.rest(0), first_qkv(sizes, a_full, normed, proj)),
+            *[functools.partial(first_attend, sizes, proj, att, b) for b in range(micro)],
+        ]
+        for i in range(len(steps) + lag):
+            if i < len(steps):
+                g.direct(*steps[i])
+            if i == 0:
+                first_norm(sizes, tokens, gain, normed)
+            if i == 0:
                 pl.semaphore_signal(
                     gate, inc=1, device_id={"section": other, "dp": me}, device_id_type=MESH
                 )
-            g.relay(*step)
-        for b in range(g.nz - 1, micro):
-            first_attend(sizes, proj, att, b)
+            if i >= lag:
+                g.relay(*steps[i - lag])
+            if i >= len(steps) - 1 and i < len(steps) + lag - 1 and chunks:
+                chunks.pop(0)()
+        for chunk in chunks:
+            chunk()
         g.rest(1)
         first_out(sizes, tokens, b_full, att, state)
         onward = across(state, state_in, 0)
@@ -643,8 +646,8 @@
     dy = norm_tangent(rows, centred, inverse, final_gain[...])
     which = lax.broadcasted_iota(jnp.int32, (count, width), 0)
     logits = dot_t(jnp.where(which < micro, y, dy).astype(BF16), head[...])
-    mean_ref[...] = logits[:micro]
-    var_ref[...] = sum(
+    mean_ref[:, 0, :] = logits[:micro]
+    var_ref[:, 0, :] = sum(
         logits[(1 + j) * micro : (2 + j) * micro] * logits[(1 + j) * micro : (2 + j) * micro]
         for j in range(tangents)
     )
@@ -667,7 +670,7 @@
         tall = hd // HEAD // 4 * BLOCK
         mean, var = pl.pallas_call(
             functools.partial(kernel, n, sizes),
-            out_shape=[jax.ShapeDtypeStruct((micro, classes), F32)] * 2,
+            out_shape=[jax.ShapeDtypeStruct((micro, 1, classes), F32)] * 2,
             in_specs=[vmem, anywhere, anywhere, anywhere, vmem, vmem, vmem],
             out_specs=[vmem, vmem],
             scratch_shapes=[
@@ -713,7 +716,7 @@
             final_gain[None],
             head.T,
         )
-        return mean[:, None, :], var[:, None, :]
+        return mean, var
 
     return shards
 

time: 85.7 us -> 77 us (0.90)
  Pallas kernels: 81.3 us -> 72.7 us
    pallas_call x1, Pallas kernels: 81.3 us -> 72.7 us  [shards(): pl.pallas_call(functools.partial(kernel, n, sizes), out_shape=[jax.ShapeD...]
    unnamed x6 -> x4, local copies, waits for them, and re-layouts: 1.94 us -> 1.87 us
where the time goes in v3:
time: 77 us; the launch traced here: 76.8 us
  Pallas kernels  72.7 us (94%)
  local copies, waits for them, and re-layouts  1.87 us (2%)
  other arithmetic  1.59 us (2%)
    pallas_call x1, Pallas kernels, shards(): pl.pallas_call(functools.partial(kernel, n, sizes), out_shape=[jax.ShapeD...  72.7 us
    unnamed x4, local copies, waits for them, and re-layouts  1.87 us
    transpose x1, other arithmetic, shards(): outs = jnp.swapaxes(jnp.concatenate([w_output, tangent_output[0]], 0), 1, 2)  1.59 us

profile of v3, /device:TPU:0, one launch (start us, length us, event | category | flops | bytes accessed | tf_op | source)
XLA Modules:
  0.0 76.8 jit_solution(4323439476196258249)
XLA Ops:
  0.6 1.6 %maximum_bitcast_fusion.outs = bf16[3,64,512]{2,1,0:T(8,128)(2,1)} fusion(bf16[2,512,64]{1,2,0:T(8,128)(2,1)} %bitcast.11, bf16[1,512,64]{1,2,0:T(8,128)(2,1)} %param.10), kind=kLoop, calls=%fused_computation | loop fusion | flops 98304 | bytes 393216 | tf_op jit(solution)/shard_map/transpose | solution.py:663
  2.2 72.7 %shard_map.95 = (f32[2,1,500]{2,1,0:T(1,128)}, f32[2,1,500]{2,1,0:T(1,128)}) custom-call(bf16[2,80,1024]{2,1,0:T(8,128)(2,1)} %bitcast.9, bf16[64,1536]{1,0:T(8,128)(2,1)} %bitcast.10, bf16[2,64,512]{2,1,0:T(8,128)(2,1)} %bitcast.12, bf16[3,64,512]{2,1,0:T(8,128)(2,1)} %maximum_bitcast_fusion.outs, f32[1,1024]{1,0:T(1,128)} %gain.1, f32[1,1024]{1,0:T(1,128)} %bitcast.13, ...), custom_call_target="tpu_custom_call" | custom-call | tf_op jit(solution)/shard_map/pallas_call | solution.py:671
  74.9 0.0 copy-start
  74.9 1.3 %copy.12 = f32[2,1,500]{2,1,0:T(1,128)} copy(f32[2,1,500]{2,1,0:T(1,128)} %get-tuple-element.4) | data formatting | bytes 8000
  76.2 0.0 copy-done
  76.2 0.6 copy.13
Async XLA Ops:
  74.9 1.3 %copy-start = (f32[2,1,500]{2,1,0:T(1,128)S(1)}, f32[2,1,500]{2,1,0:T(1,128)}, u32[]{:S(2)}) copy-start(f32[2,1,500]{2,1,0:T(1,128)} %get-tuple-element.5) | copy-start | bytes 12004
